TPU v7x, 32 devices: a whole 2x2x4 slice. The times are simulated.
32 devices in a mesh: expert: 8 (over z, y), tensor: 4 (over x, core).
Axes of the slice: x: 2, y: 2, z: 4, core: 2. Of those that a mesh axis runs over, the one named last changes fastest.
Arguments:
- tokens: bfloat16 [1024, 3072], P('expert', 'tensor'), may hold values from -6 to 6
- expert_ids: int32 [1024, 2], P('expert'), may hold values from 0 to 7, all different within a row; in each aligned block of 128 rows (0 to 127, 128 to 255, ...) at most 48 rows name the same one
- joined_weight: bfloat16 [8, 3072, 2, 16384], P('expert', 'tensor'), may hold values from -0.109375 to 0.109375
Outputs:
- hidden: bfloat16 [1024, 2, 1, 16384], P('expert', None, None, 'tensor')
Inputs may be any that keep to these rules, and one draw needn't show every extreme that they name: `expert_ids`: each row names 2 different experts. Among the rows of one device (each aligned block of 128 rows) no expert is named by more than 48 rows, and in some blocks one expert is named by exactly 48 rows.
All inputs are finite; a program needn't handle non-finite values.
Results may differ from a plain program's by a relative error of at most 0.001.
Values may be sent and summed in bfloat16 or wider, within the bound.
A program may use at most 256 MiB of HBM per device.

v0:
```python
import functools

import jax
import jax.numpy as jnp
from jax import lax
from jax.experimental import pallas as pl
from jax.experimental.pallas import tpu as pltpu
from jax.sharding import PartitionSpec as P

E = 8
TOP = 2
CAP = 48
TOP_CODE = 32767.0
SLOTS = 4
LAG = 2


def remote(src, dst, send, recv, **where):
    return pltpu.make_async_remote_copy(
        src_ref=src,
        dst_ref=dst,
        send_sem=send,
        recv_sem=recv,
        device_id=where,
        device_id_type=pl.DeviceIdType.MESH,
    )


def kernel(
    groups, blocks, half, width, chunk, sub,
    placed, pick, weight, out,
    x, w, part, qs, qr, scale_s, scale_r, base, act, ret, stage,
    tok_send, tok_recv, fwd_send, fwd_recv,
    w_local, w_send, w_recv, q_send, q_recv, s_send, s_recv,
    act_send, act_recv, out_sem, credit,
):
    copies = blocks // E
    chips = groups // 2
    rows = blocks * CAP
    count = half // chunk
    parts = chunk // sub
    subs = half // sub
    far = (chips - 1) * count
    total = chips * count
    e, t = lax.axis_index("expert"), lax.axis_index("tensor")
    core, chip = lax.rem(t, 2), lax.div(t, 2)
    partner = chip * 2 + 1 - core
    tokens = pick.shape[1]

    def peer(d):
        return lax.rem(e + d, blocks)

    def across(o):
        return lax.rem(chip + o, chips) * 2 + core

    barrier = pltpu.get_barrier_semaphore()

    def greet(**where):
        pl.semaphore_signal(barrier, inc=1, device_id=where, device_id_type=pl.DeviceIdType.MESH)

    for d in range(1, blocks):
        greet(expert=peer(d))
    greet(tensor=partner)
    for o in range(1, chips):
        greet(tensor=across(o))
    pl.semaphore_wait(barrier, blocks - 1 + 1 + chips - 1)

    def bring(k, slot):
        target = lax.rem(chip + 1 + lax.div(k, count), chips)
        j = lax.rem(k, count)
        mine = pl.multiple_of((target * 2 + core) * half + j * chunk, 128)
        theirs = pl.multiple_of((target * 2 + 1 - core) * half + j * chunk, 128)
        here = pltpu.make_async_copy(
            weight.at[0, :, :, pl.ds(mine, chunk)], w.at[slot, 0], w_local.at[slot]
        )
        there = remote(
            weight.at[0, :, :, pl.ds(theirs, chunk)], w.at[slot, 1],
            w_send.at[slot], w_recv.at[slot], tensor=partner,
        )
        return here, there

    def start_weights(k, slot):
        here, there = bring(k, slot)
        there.start()
        here.start()

    token_copies = []
    for d in range(1, blocks):
        copy = remote(
            placed.at[lax.div(peer(d), copies)], x.at[0, e],
            tok_send.at[d], tok_recv.at[e], expert=peer(d),
        )
        copy.start()
        token_copies.append(copy)
    for k in range(min(SLOTS, total)):
        start_weights(k, k)
    x[0, e] = placed[lax.div(e, copies)]

    forwards = []
    for d in range(blocks):
        source = lax.rem(e + blocks - d, blocks)
        src = x.at[0, source]
        if d == 0:
            src = placed.at[lax.div(e, copies)]
        else:
            remote(
                x.at[0, source], x.at[0, source], tok_send.at[0], tok_recv.at[source],
                expert=source,
            ).wait_recv()
        copy = remote(
            src, x.at[1, source], fwd_send.at[source], fwd_recv.at[source], tensor=partner
        )
        copy.start()
        forwards.append(copy)
    for copy in forwards:
        copy.wait_recv()

    def products(k, use):
        slot = lax.rem(k, SLOTS)
        here, there = bring(k, slot)
        here.wait()
        there.wait_recv()
        own = x[0].reshape(rows, width)
        other = x[1].reshape(rows, width)
        mine = jnp.swapaxes(w[slot, 0], 0, 1)
        theirs = jnp.swapaxes(w[slot, 1], 0, 1)
        for c in range(2):
            use(
                c,
                jnp.dot(own, mine[c], preferred_element_type=jnp.float32)
                + jnp.dot(other, theirs[c], preferred_element_type=jnp.float32),
            )

        @pl.when(k + SLOTS < total)
        def _():
            pl.semaphore_signal(
                credit, inc=1, device_id={"tensor": partner}, device_id_type=pl.DeviceIdType.MESH
            )

        @pl.when(jnp.logical_and(k >= 1, k - 1 + SLOTS < total))
        def _():
            before = lax.rem(k + SLOTS - 1, SLOTS)
            bring(k - 1, before)[1].wait_send()
            pl.semaphore_wait(credit, 1)
            start_weights(k - 1 + SLOTS, before)

    def code_copies(o, q):
        return (
            remote(qs.at[q], qr.at[q], q_send.at[q], q_recv.at[q], tensor=across(o)),
            remote(scale_s.at[q], scale_r.at[q], s_send.at[q], s_recv.at[q], tensor=across(o)),
        )

    def far_step(k, carry):
        def use(c, value):
            part[c] = value

        products(k, use)
        o = 1 + lax.div(k, count)
        j = lax.rem(k, count)
        for h in range(parts):
            q = (o - 1) * subs + j * parts + h
            for c in range(2):
                value = part[c, :, h * sub : (h + 1) * sub]
                top = jnp.maximum(jnp.max(jnp.abs(value), axis=0, keepdims=True), 1e-30)
                code = jnp.round(value * (TOP_CODE / top)).astype(jnp.int32).astype(jnp.int16)
                qs[q, :, c * sub : (c + 1) * sub] = code
                scale_s[q, :, c * sub : (c + 1) * sub] = top * (1.0 / TOP_CODE)
            for copy in code_copies(o, q):
                copy.start()
        return carry

    def near_step(k, carry):
        j = lax.rem(k, count)

        def use(c, value):
            for h in range(parts):
                base[j * parts + h, c] = value[:, h * sub : (h + 1) * sub]

        products(k, use)
        return carry

    lax.fori_loop(0, far, far_step, 0)
    lax.fori_loop(far, total, near_step, 0)

    def act_copy(s, d):
        return remote(
            act.at[s, peer(d)], ret.at[s, lax.rem(e, copies), lax.div(e, copies)],
            act_send.at[s], act_recv.at[s], expert=peer(d),
        )

    def act_all(s):
        every = act.at[s, pl.ds(0, blocks - 1)]
        return remote(every, every, act_send.at[s], act_recv.at[s], expert=peer(1))

    def out_copy(s):
        return pltpu.make_async_copy(
            stage.at[s], out.at[:, :, :, pl.ds(pl.multiple_of(s * sub, 128), sub)], out_sem.at[s]
        )

    def finish(s):
        act_all(s).wait_recv()
        for r in range(copies):
            got = ret[s, r].reshape(E * CAP, sub)
            picked = [
                jnp.dot(pick[k], got, preferred_element_type=jnp.float32).astype(jnp.bfloat16)
                for k in range(TOP)
            ]
            stage[s, :, r] = jnp.swapaxes(jnp.stack(picked), 0, 1)
        out_copy(s).start()

    def receive(s, carry):
        for o in range(1, chips):
            for copy in code_copies(o, (o - 1) * subs + s):
                copy.wait_recv()
        for b in range(blocks):
            line = slice(b * CAP, (b + 1) * CAP)
            gate, up = base[s, 0, line], base[s, 1, line]
            for o in range(1, chips):
                q = (o - 1) * subs + s
                gate = gate + qr[q, line, :sub].astype(jnp.int32).astype(jnp.float32) * scale_r[q, :, :sub]
                up = up + qr[q, line, sub:].astype(jnp.int32).astype(jnp.float32) * scale_r[q, :, sub:]
            act[s, b] = (gate / (1.0 + jnp.exp(-gate)) * up).astype(jnp.bfloat16)
        for d in range(1, blocks):
            act_copy(s, d).start()
        ret[s, lax.rem(e, copies), lax.div(e, copies)] = act[s, e]

        @pl.when(s >= LAG)
        def _():
            finish(s - LAG)

        return carry

    lax.fori_loop(0, subs, receive, 0)
    for s in range(max(0, subs - LAG), subs):
        finish(s)

    for copy in token_copies:
        copy.wait_send()
    for copy in forwards:
        copy.wait_send()
    for k in range(max(0, total - SLOTS), total):
        bring(k, k % SLOTS)[1].wait_send()
    for o in range(1, chips):

        def sent(s, carry):
            for copy in code_copies(o, (o - 1) * subs + s):
                copy.wait_send()
            return carry

        lax.fori_loop(0, subs, sent, 0)

    def done(s, carry):
        act_all(s).wait_send()
        out_copy(s).wait()
        return carry

    lax.fori_loop(0, subs, done, 0)


def local(tokens, expert_ids, joined_weight):
    groups = lax.axis_size("tensor")
    blocks = lax.axis_size("expert")
    copies = blocks // E
    chips = groups // 2
    half = joined_weight.shape[3] // groups
    tok_count, width = tokens.shape
    chunk = 512 if half % 512 == 0 else half
    sub = 256 if chunk % 256 == 0 else chunk
    subs = half // sub
    rows = blocks * CAP
    codes = (chips - 1) * subs

    flat_ids = expert_ids.reshape(-1)
    chosen = (flat_ids[:, None] == jnp.arange(E, dtype=jnp.int32)[None, :]).astype(jnp.int32)
    earlier = jnp.cumsum(chosen, axis=0) - chosen
    position = jnp.sum(earlier * chosen, axis=1)
    slot_index = flat_ids * CAP + position
    pick = (slot_index[:, None] == jnp.arange(E * CAP, dtype=jnp.int32)[None, :]).astype(
        jnp.bfloat16
    )
    pick = pick.reshape(tok_count, TOP, E * CAP)
    placed = lax.dot_general(
        pick.sum(axis=1), tokens, (((0,), (0,)), ((), ())), preferred_element_type=jnp.float32
    )
    placed = placed.astype(jnp.bfloat16).reshape(E, CAP, width)
    pick = pick.transpose(1, 0, 2)

    dma = pltpu.SemaphoreType.DMA
    vmem = pl.BlockSpec(memory_space=pltpu.VMEM)
    hbm = pl.BlockSpec(memory_space=pl.ANY)
    result = pl.pallas_call(
        functools.partial(kernel, groups, blocks, half, width, chunk, sub),
        out_shape=jax.ShapeDtypeStruct((tok_count, copies, TOP, half), jnp.bfloat16),
        in_specs=[vmem, vmem, hbm],
        out_specs=hbm,
        scratch_shapes=[
            pltpu.VMEM((2, blocks, CAP, width), jnp.bfloat16),
            pltpu.VMEM((SLOTS, 2, width, 2, chunk), jnp.bfloat16),
            pltpu.VMEM((2, rows, chunk), jnp.float32),
            pltpu.VMEM((codes, rows, 2 * sub), jnp.int16),
            pltpu.VMEM((codes, rows, 2 * sub), jnp.int16),
            pltpu.VMEM((codes, 1, 2 * sub), jnp.float32),
            pltpu.VMEM((codes, 1, 2 * sub), jnp.float32),
            pltpu.VMEM((subs, 2, rows, sub), jnp.float32),
            pltpu.VMEM((subs, blocks, CAP, sub), jnp.bfloat16),
            pltpu.VMEM((subs, copies, E, CAP, sub), jnp.bfloat16),
            pltpu.VMEM((subs, tok_count, copies, TOP, sub), jnp.bfloat16),
            dma((blocks,)), dma((blocks,)), dma((blocks,)), dma((blocks,)),
            dma((SLOTS,)), dma((SLOTS,)), dma((SLOTS,)),
            dma((codes,)), dma((codes,)), dma((codes,)), dma((codes,)),
            dma((subs,)), dma((subs,)), dma((subs,)),
            pltpu.SemaphoreType.REGULAR,
        ],
        compiler_params=pltpu.CompilerParams(
            collective_id=0, has_side_effects=True, vmem_limit_bytes=66 * 1024 * 1000
        ),
        name="experts",
    )(placed, pick, joined_weight)
    return result.transpose(0, 2, 1, 3)


def solution(mesh):
    placed = (P("expert", "tensor"), P("expert", None), P("expert", "tensor", None, None))
    return jax.shard_map(
        local,
        mesh=mesh,
        in_specs=placed,
        out_specs=P("expert", None, None, "tensor"),
        check_vma=False,
    )
```

profile of v0, /device:TPU:0, one launch (start us, length us, event | category | flops | bytes accessed | tf_op | source)
XLA Modules:
  0.0 178.9 jit_solution(5970066041530185160)
XLA Ops:
  0.0 0.8 copy.19
  0.8 0.1 eq.52
  0.9 0.1 eq.48
  1.1 0.6 reduce-window.6
  1.7 0.2 slice_reduce_fusion
  1.9 0.1 fusion.4
  2.0 0.1 reduce_sum.24
  2.2 0.1 copy.21
  2.2 0.7 multiply_add_fusion
  2.9 0.1 fusion.2
  3.0 0.8 fusion.1.pick
  3.8 2.1 %convolution_convert_fusion = bf16[384,768]{1,0:T(8,128)(2,1)} fusion(bf16[128,384]{1,0:T(8,128)(2,1)S(1)} %fusion.2, bf16[128,768]{1,0:T(8,128)(2,1)} %param.3), kind=kOutput, calls=%fused_computation | convolution fusion | flops 75792384 | bytes 884736 | tf_op jit(solution)/shard_map/dot_general | solution.py:282
  5.9 168.0 %experts.1 = bf16[128,1,2,4096]{3,2,1,0:T(2,128)(2,1)} custom-call(bf16[8,48,768]{2,1,0:T(8,128)(2,1)} %bitcast.16, bf16[2,128,384]{2,1,0:T(8,128)(2,1)} %fusion.1.pick, bf16[1,768,2,16384]{3,2,1,0:T(2,128)(2,1)} %weight.1), custom_call_target="tpu_custom_call" | custom-call | tf_op jit(solution)/shard_map/experts/pallas_call | solution.py:291
  174.0 4.9 %copy.24 = bf16[128,2,1,4096]{3,1,2,0:T(2,128)(2,1)} copy(bf16[128,2,1,4096]{3,1,2,0:T(2,128)(2,1)} %bitcast.15) | data formatting | bytes 4194304
  (3 shorter events, 0.0 us)
where the time goes:
time: 179 us
  Pallas kernels  168 us (94%)
  local copies, waits for them, and re-layouts  6.4 us (4%)
  other arithmetic  2.32 us (1%)
  matrix products  2.09 us (1%)
    pallas_call x1, Pallas kernels, local(): pl.pallas_call(functools.partial(kernel, groups, blocks, half, width, chu...  168 us
    unnamed x2, local copies, waits for them, and re-layouts  5.71 us

commit v1 on v0

v1 whole, which is shorter than its diff:
```python
import functools

import jax
import jax.numpy as jnp
from jax import lax
from jax.experimental import pallas as pl
from jax.experimental.pallas import tpu as pltpu
from jax.sharding import PartitionSpec as P

E = 8
TOP = 2
CAP = 48
TOP_CODE = 32767.0
SLOTS = 6
OPEN = 5
SPLIT = 3
LAST = 2
MESH = pl.DeviceIdType.MESH


def remote(src, dst, send, recv, **where):
    return pltpu.make_async_remote_copy(
        src_ref=src,
        dst_ref=dst,
        send_sem=send,
        recv_sem=recv,
        device_id=where,
        device_id_type=MESH,
    )


def flipped(index, distance):
    bit = 1
    while bit <= distance:
        if distance & bit:
            index = index + bit - 2 * bit * lax.rem(lax.div(index, bit), 2)
        bit *= 2
    return index


def kernel(
    groups, blocks, half, width, chunk,
    tokens, ids, weight, out,
    tok_v, ids_v, placed, pick, x, w, qs, qr, scale_s, scale_r, base, act, ret, stage,
    in_sem, tok_send, tok_recv, fwd_send, fwd_recv,
    w_local, w_send, w_recv, q_send, q_recv, s_send, s_recv,
    act_send, act_recv, out_sem, credit,
):
    copies = blocks // E
    chips = groups // 2
    near = blocks // 2
    count = half // chunk
    far = (chips - 1) * count
    total = chips * count
    e, t = lax.axis_index("expert"), lax.axis_index("tensor")
    core, chip = lax.rem(t, 2), lax.div(t, 2)
    partner = chip * 2 + 1 - core
    tok_count = tok_v.shape[0]
    peers = [flipped(e, d) for d in range(blocks)]

    def across(o):
        return lax.rem(chip + o, chips) * 2 + core

    barrier = pltpu.get_barrier_semaphore()

    def greet(**where):
        pl.semaphore_signal(barrier, inc=1, device_id=where, device_id_type=MESH)

    ids_in = pltpu.make_async_copy(ids, ids_v, in_sem.at[0])
    tokens_in = pltpu.make_async_copy(tokens, tok_v, in_sem.at[1])
    ids_in.start()
    tokens_in.start()
    for d in range(1, blocks):
        greet(expert=peers[d])
    greet(tensor=partner)
    for o in range(1, chips):
        greet(tensor=across(o))

    opening = min(OPEN, far)
    split = min(SPLIT, opening)
    last = min(LAST, far - opening)
    mixed = chips == 2 and count > OPEN + LAST
    middle = far - opening - last if mixed else 0

    def own_apart(k):
        return jnp.logical_or(k < split, k >= far - last)

    def piece(n):
        if not mixed:
            return n
        m = n - opening
        turn = jnp.where(lax.rem(m, 2) == 0, opening + lax.div(m, 2), far + lax.div(m, 2))
        rest = jnp.where(m < 2 * middle + last, opening + m - middle, far + m - middle - last)
        return jnp.where(m < 0, n, jnp.where(m < 2 * middle, turn, rest))

    def bring(n, slot):
        k = piece(n)
        target = lax.rem(chip + 1 + lax.div(k, count), chips)
        j = lax.rem(k, count)
        mine = pl.multiple_of((target * 2 + core) * half + j * chunk, 128)
        theirs = pl.multiple_of((target * 2 + 1 - core) * half + j * chunk, 128)
        here = pltpu.make_async_copy(
            weight.at[0, :, :, pl.ds(mine, chunk)], w.at[slot, 0], w_local.at[slot]
        )
        there = remote(
            weight.at[0, :, :, pl.ds(theirs, chunk)], w.at[slot, 1],
            w_send.at[slot], w_recv.at[slot], tensor=partner,
        )
        return here, there

    ahead = min(SLOTS, total)
    for k in range(ahead):
        bring(k, k)[0].start()

    pl.semaphore_wait(barrier, blocks - 1 + 1 + chips - 1)
    bring(0, 0)[1].start()

    ids_in.wait()
    named = lax.broadcasted_iota(jnp.int32, (E, tok_count), 0)
    chosen = [(named == ids_v[k : k + 1, :]).astype(jnp.float32) for k in range(TOP)]
    before = lax.broadcasted_iota(jnp.int32, (tok_count, tok_count), 0) < lax.broadcasted_iota(
        jnp.int32, (tok_count, tok_count), 1
    )
    seen = jnp.dot(
        sum(chosen).astype(jnp.bfloat16),
        before.astype(jnp.float32).astype(jnp.bfloat16),
        preferred_element_type=jnp.float32,
    )
    line = lax.broadcasted_iota(jnp.int32, (E * CAP, tok_count), 0)
    taken = []
    for k in range(TOP):
        position = jnp.sum(seen * chosen[k], axis=0, keepdims=True).astype(jnp.int32)
        taken.append((line == ids_v[k : k + 1, :] * CAP + position).astype(jnp.float32))
        seen = seen + chosen[k]
    tokens_in.wait()
    placed[...] = (
        jnp.dot(sum(taken).astype(jnp.bfloat16), tok_v[...], preferred_element_type=jnp.float32)
        .astype(jnp.bfloat16)
        .reshape(E, CAP, width)
    )

    def token_copy(d):
        return remote(
            placed.at[lax.div(peers[d], copies)], x.at[0, d],
            tok_send.at[d], tok_recv.at[d], expert=peers[d],
        )

    def forward(d):
        src = x.at[0, d] if d else placed.at[lax.div(e, copies)]
        return remote(src, x.at[1, d], fwd_send.at[d], fwd_recv.at[d], tensor=partner)

    forward(0).start()
    for d in range(1, near):
        token_copy(d).start()
    for k in range(1, min(SPLIT, ahead)):
        bring(k, k)[1].start()
    x[0, 0] = placed[lax.div(e, copies)]

    def products(slot, first, some, use):
        own = x[0, pl.ds(first, some)].reshape(some * CAP, width)
        other = x[1, pl.ds(first, some)].reshape(some * CAP, width)
        mine = jnp.swapaxes(w[slot, 0], 0, 1)
        theirs = jnp.swapaxes(w[slot, 1], 0, 1)
        for c in range(2):
            use(
                c,
                jnp.dot(own, mine[c], preferred_element_type=jnp.float32)
                + jnp.dot(other, theirs[c], preferred_element_type=jnp.float32),
            )

    def await_weights(k):
        here, there = bring(k, lax.rem(k, SLOTS))
        here.wait()
        there.wait_recv()

    def release(k):
        @pl.when(k + SLOTS < total)
        def _():
            pl.semaphore_signal(credit, inc=1, device_id={"tensor": partner}, device_id_type=MESH)

        @pl.when(jnp.logical_and(k >= 1, k - 1 + SLOTS < total))
        def _():
            old = lax.rem(k + SLOTS - 1, SLOTS)
            here, there = bring(k - 1 + SLOTS, old)
            there.wait_send()
            pl.semaphore_wait(credit, 1)
            there.start()
            here.start()

    def code_copies(k, at, first, some):
        o = 1 + lax.div(k, count)
        span = pl.ds(pl.multiple_of(first * CAP, 16), some * CAP)
        return (
            remote(qs.at[k, span], qr.at[k, span], q_send.at[at, k], q_recv.at[at, k], tensor=across(o)),
            remote(scale_s.at[at, k], scale_r.at[at, k], s_send.at[at, k], s_recv.at[at, k], tensor=across(o)),
        )

    def send(n, k, at, first, some):
        def use(c, value):
            top = jnp.maximum(jnp.max(jnp.abs(value), axis=0, keepdims=True), 1e-30)
            code = jnp.round(value * (TOP_CODE / top)).astype(jnp.int32).astype(jnp.int16)
            span = pl.ds(pl.multiple_of(first * CAP, 16), some * CAP)
            qs[k, span, c * chunk : (c + 1) * chunk] = code
            scale_s[at, k, :, c * chunk : (c + 1) * chunk] = top * (1.0 / TOP_CODE)

        products(lax.rem(n, SLOTS), first, some, use)
        for copy in code_copies(k, at, first, some):
            copy.start()

    def own_step(k, carry):
        await_weights(k)
        send(k, k, 2, 0, 1)
        return carry

    def near_rows(k, carry):
        send(k, k, 0, 1, near - 1)
        return carry

    def near_part(k, carry):
        await_weights(k)
        send(k, k, 0, 0, near)
        return carry

    def far_part(k, carry):
        send(k, k, 1, near, blocks - near)
        release(k)
        return carry

    def both(n, k):
        await_weights(n)

        def half_of_rows(i, carry):
            r = 1 - i
            send(n, k, r, r * near, near)
            return carry

        lax.fori_loop(0, 2, half_of_rows, 0)
        release(n)

    def others(i, carry):
        n = opening + 2 * middle + i if mixed else far - last + i
        await_weights(n)
        send(n, far - last + i, 1, near, blocks - near)
        send(n, far - last + i, 0, 1, near - 1)
        return carry

    def own_late(i, carry):
        n = opening + 2 * middle + i if mixed else far - last + i
        send(n, far - last + i, 2, 0, 1)
        release(n)
        return carry

    def own_chip(n, j):
        await_weights(n)

        def use(c, value):
            base[lax.rem(j, base.shape[0]), c] = value

        products(lax.rem(n, SLOTS), 0, blocks, use)
        release(n)

    forward(0).wait_recv()
    lax.fori_loop(0, min(1, split), own_step, 0)
    for d in range(1, near):
        token_copy(d).wait_recv()
        forward(d).start()
    for d in range(near, blocks):
        token_copy(d).start()
    for k in range(split, min(opening, ahead)):
        bring(k, k)[1].start()
    lax.fori_loop(1, split, own_step, 0)
    for d in range(1, near):
        forward(d).wait_recv()
    lax.fori_loop(0, split, near_rows, 0)
    lax.fori_loop(split, opening, near_part, 0)
    for k in range(TOP):
        pick[k] = taken[k].T.astype(jnp.bfloat16)
    for d in range(near, blocks):
        token_copy(d).wait_recv()
        forward(d).start()
    for k in range(opening, ahead):
        bring(k, k)[1].start()
    for d in range(near, blocks):
        forward(d).wait_recv()
    lax.fori_loop(0, opening, far_part, 0)
    def act_copy(s, d):
        return remote(
            act.at[s, d], ret.at[s, lax.rem(e, copies), lax.div(e, copies)],
            act_send.at[s], act_recv.at[s], expert=peers[d],
        )

    def act_all(s):
        every = act.at[s, pl.ds(0, blocks - 1)]
        return remote(every, every, act_send.at[s], act_recv.at[s], expert=peers[1])

    def out_copy(s):
        return pltpu.make_async_copy(
            stage.at[s], out.at[:, :, :, pl.ds(pl.multiple_of(s * chunk, 128), chunk)], out_sem.at[s]
        )

    def finish(s, carry):
        act_all(s).wait_recv()
        for r in range(copies):
            got = ret[s, r].reshape(E * CAP, chunk)
            picked = [
                jnp.dot(pick[k], got, preferred_element_type=jnp.float32).astype(jnp.bfloat16)
                for k in range(TOP)
            ]
            stage[s, :, r] = jnp.swapaxes(jnp.stack(picked), 0, 1)
        out_copy(s).start()
        return carry

    def activate(s, b):
        line = slice(b * CAP, (b + 1) * CAP)
        at = lax.rem(s, base.shape[0])
        gate, up = base[at, 0, line], base[at, 1, line]
        for o in range(1, chips):
            k = (o - 1) * count + s
            at = b // near if b else jnp.where(own_apart(k), 2, 0)
            scale = scale_r[at, k]
            gate = gate + qr[k, line, :chunk].astype(jnp.int32).astype(jnp.float32) * scale[:, :chunk]
            up = up + qr[k, line, chunk:].astype(jnp.int32).astype(jnp.float32) * scale[:, chunk:]
        return (gate / (1.0 + jnp.exp(-gate)) * up).astype(jnp.bfloat16)

    def hand_back(s, first, end):
        for d in range(first, end):
            act[s, d] = activate(s, d)
            act_copy(s, d).start()

    def keep(s):
        ret[s, lax.rem(e, copies), lax.div(e, copies)] = activate(s, 0)

    def await_codes(k, at, first, some):
        for copy in code_copies(k, at, first, some):
            copy.wait_recv()

    def await_near(k):
        @pl.when(own_apart(k))
        def _():
            await_codes(k, 2, 0, 1)
            await_codes(k, 0, 1, near - 1)

        @pl.when(jnp.logical_not(own_apart(k)))
        def _():
            await_codes(k, 0, 0, near)

    def whole(s, carry):
        for o in range(1, chips):
            k = (o - 1) * count + s
            await_codes(k, 1, near, blocks - near)
            await_near(k)
        hand_back(s, 1, blocks)
        keep(s)
        return carry

    def nearer(s, carry):
        await_near(s)
        hand_back(s, 1, near)
        keep(s)
        return carry

    def farther(s, carry):
        await_codes(s, 1, near, blocks - near)
        hand_back(s, near, blocks)
        return carry

    def received(s):
        farther(s, 0)

        @pl.when(s >= 2)
        def _():
            finish(s - 2, 0)

        nearer(s, 0)

    def turn(i, carry):
        both(opening + 2 * i, opening + i)
        own_chip(opening + 2 * i + 1, i)
        received(i)
        return carry

    def drain(i, carry):
        own_chip(far + i, i)
        received(i)
        return carry

    def received_last(s, carry):
        own_chip(far + s, s)
        farther(s, 0)
        finish(s - 2, 0)
        await_codes(s, 0, 1, near - 1)
        hand_back(s, 1, near)
        return carry

    def received_own(s, carry):
        await_codes(s, 2, 0, 1)
        keep(s)
        return finish(s, 0)

    if mixed:
        lax.fori_loop(0, middle, turn, 0)
        lax.fori_loop(0, last, others, 0)
        lax.fori_loop(0, last, own_late, 0)
        lax.fori_loop(middle, count - last, drain, 0)
        lax.fori_loop(count - last, count, received_last, 0)
        lax.fori_loop(count - last, count, received_own, 0)
    else:

        def sent_whole(k, carry):
            both(k, k)
            return carry

        def own_whole(j, carry):
            own_chip(far + j, j)
            return carry

        lax.fori_loop(opening, far - last, sent_whole, 0)
        lax.fori_loop(0, last, others, 0)
        lax.fori_loop(0, last, own_late, 0)
        lax.fori_loop(0, count, own_whole, 0)
        lax.fori_loop(0, count, whole, 0)
        lax.fori_loop(0, count, finish, 0)

    for d in range(1, blocks):
        token_copy(d).wait_send()
    for d in range(blocks):
        forward(d).wait_send()
    for k in range(max(0, total - SLOTS), total):
        bring(k, k % SLOTS)[1].wait_send()

    def sent(k, carry):
        for copy in code_copies(k, 1, near, blocks - near):
            copy.wait_send()

        @pl.when(own_apart(k))
        def _():
            for copy in code_copies(k, 0, 1, near - 1) + code_copies(k, 2, 0, 1):
                copy.wait_send()

        @pl.when(jnp.logical_not(own_apart(k)))
        def _():
            for copy in code_copies(k, 0, 0, near):
                copy.wait_send()

        return carry

    lax.fori_loop(0, far, sent, 0)

    def done(s, carry):
        act_all(s).wait_send()
        out_copy(s).wait()
        return carry

    lax.fori_loop(0, count, done, 0)


def local(tokens, expert_ids, joined_weight):
    groups = lax.axis_size("tensor")
    blocks = lax.axis_size("expert")
    copies = blocks // E
    chips = groups // 2
    half = joined_weight.shape[3] // groups
    tok_count, width = tokens.shape
    chunk = 256 if half % 256 == 0 else half
    count = half // chunk
    rows = blocks * CAP
    codes = (chips - 1) * count

    dma = pltpu.SemaphoreType.DMA
    hbm = pl.BlockSpec(memory_space=pl.ANY)
    result = pl.pallas_call(
        functools.partial(kernel, groups, blocks, half, width, chunk),
        out_shape=jax.ShapeDtypeStruct((tok_count, copies, TOP, half), jnp.bfloat16),
        in_specs=[hbm, hbm, hbm],
        out_specs=hbm,
        scratch_shapes=[
            pltpu.VMEM((tok_count, width), jnp.bfloat16),
            pltpu.VMEM((TOP, tok_count), jnp.int32),
            pltpu.VMEM((E, CAP, width), jnp.bfloat16),
            pltpu.VMEM((TOP, tok_count, E * CAP), jnp.bfloat16),
            pltpu.VMEM((2, blocks, CAP, width), jnp.bfloat16),
            pltpu.VMEM((SLOTS, 2, width, 2, chunk), jnp.bfloat16),
            pltpu.VMEM((codes, rows, 2 * chunk), jnp.int16),
            pltpu.VMEM((codes, rows, 2 * chunk), jnp.int16),
            pltpu.VMEM((3, codes, 1, 2 * chunk), jnp.float32),
            pltpu.VMEM((3, codes, 1, 2 * chunk), jnp.float32),
            pltpu.VMEM((2 if chips == 2 and count > OPEN + LAST else count, 2, rows, chunk), jnp.float32),
            pltpu.VMEM((count, blocks, CAP, chunk), jnp.bfloat16),
            pltpu.VMEM((count, copies, E, CAP, chunk), jnp.bfloat16),
            pltpu.VMEM((count, tok_count, copies, TOP, chunk), jnp.bfloat16),
            dma((2,)), dma((blocks,)), dma((blocks,)), dma((blocks,)), dma((blocks,)),
            dma((SLOTS,)), dma((SLOTS,)), dma((SLOTS,)),
            dma((3, codes)), dma((3, codes)), dma((3, codes)), dma((3, codes)),
            dma((count,)), dma((count,)), dma((count,)),
            pltpu.SemaphoreType.REGULAR,
        ],
        compiler_params=pltpu.CompilerParams(
            collective_id=0, has_side_effects=True, vmem_limit_bytes=51 * 1024 * 1024
        ),
        name="experts",
    )(tokens, expert_ids.T, joined_weight)
    return result.transpose(0, 2, 1, 3)


def solution(mesh):
    placed = (P("expert", "tensor"), P("expert", None), P("expert", "tensor", None, None))
    return jax.shard_map(
        local,
        mesh=mesh,
        in_specs=placed,
        out_specs=P("expert", None, None, "tensor"),
        check_vma=False,
    )
```

time: 179 us -> 159 us (0.89)
  Pallas kernels: 168 us -> 156 us
  local copies, waits for them, and re-layouts: 6.4 us -> 2.93 us
  other arithmetic: 2.32 us -> 0 us
  matrix products: 2.09 us -> 0 us
    pallas_call x1, Pallas kernels: 168 us -> 156 us  [local(): pl.pallas_call(functools.partial(kernel, groups, blocks, half, width, chu...]
    unnamed x2 -> x5, local copies, waits for them, and re-layouts: 5.71 us -> 2.93 us
    dot_general x1 -> x0, matrix products: 2.09 us -> none  [local(): lax.dot_general(pick.sum(axis=1), tokens, (((0,), (0,)), ((), ())), prefe...]
where the time goes in v1:
time: 159 us
  Pallas kernels  156 us (98%)
  local copies, waits for them, and re-layouts  2.93 us (2%)
    pallas_call x1, Pallas kernels, local(): pl.pallas_call(functools.partial(kernel, groups, blocks, half, width, chu...  156 us

profile of v1, /device:TPU:0, one launch (start us, length us, event | category | flops | bytes accessed | tf_op | source)
XLA Modules:
  0.0 158.9 jit_solution(17051982279429625546)
XLA Ops:
  0.0 0.0 copy-start
  0.0 0.9 copy-done
  0.9 0.0 copy-start.1
  0.9 0.7 copy-done.1
  1.6 156.0 %experts.1 = bf16[128,1,2,4096]{3,2,1,0:T(2,128)(2,1)S(1)} custom-call(bf16[128,768]{1,0:T(8,128)(2,1)S(1)} %copy-done, s32[2,128]{1,0:T(2,128)S(1)} %bitcast.5, bf16[1,768,2,16384]{3,2,1,0:T(2,128)(2,1)} %weight.1), custom_call_target="tpu_custom_call" | custom-call | tf_op jit(solution)/shard_map/experts/pallas_call | solution.py:471
  157.6 1.3 copy.6
Async XLA Ops:
  0.0 0.9 copy-start
  0.9 0.7 copy-start.1
